TPU v7x, 256 devices: a whole 4x4x8 slice. The times are simulated.
256 devices in a mesh: ens: 4 (over y), fsdp: 16 (over z, core), model: 4 (over x).
Axes of the slice: x: 4, y: 4, z: 8, core: 2. Of those that a mesh axis runs over, the one named last changes fastest.
Arguments:
- weight_gate: bfloat16 [8192, 8192], P(('ens', 'fsdp'), 'model'), parts along dimension 0, may hold values from -0.125 to 0.125
- low_gate: bfloat16 [8192, 32], P(('ens', 'fsdp')), parts along dimension 0, may hold values from -0.125 to 0.125
- high_gate: bfloat16 [128, 8192], P('ens', 'model'), parts along dimension 0, may hold values from -1 to 1
- weight_up: bfloat16 [8192, 8192], P(('ens', 'fsdp'), 'model'), parts along dimension 0, may hold values from -0.125 to 0.125
- low_up: bfloat16 [8192, 32], P(('ens', 'fsdp')), parts along dimension 0, may hold values from -0.125 to 0.125
- high_up: bfloat16 [128, 8192], P('ens', 'model'), parts along dimension 0, may hold values from -1 to 1
- norm_train: float32 [8192], P(('ens', 'fsdp', 'model')), parts along dimension 0, may hold values from 0.25 to 1.75
- norm_step: float32 [8192], P(('ens', 'fsdp', 'model')), parts along dimension 0, may hold values from -0.3 to 0.3
Outputs:
- final_gate: bfloat16 [32768, 2048], P(('ens', 'model')), parts along dimension 0
- final_up: bfloat16 [32768, 2048], P(('ens', 'model')), parts along dimension 0
- serve_norm: bfloat16 [8192], P('ens'), parts along dimension 0
There are 4 independent parts, one for each index of `ens`. A program takes and returns all parts, laid end to end along the dimension named above; each array names one. Nothing has to cross between parts.
All inputs are finite; a program needn't handle non-finite values.
Results may differ from a plain program's by a relative error of at most 0.001.
Values may be sent and summed in bfloat16 or wider, within the bound.
A program may use at most 128 MiB of HBM per device.

v0:
```python
import jax
import jax.numpy as jnp
from jax import lax
from jax.sharding import PartitionSpec as P

mix_rate = 2.0


def sent_to_all(shard, axis):
    copies = jnp.broadcast_to(shard, (lax.axis_size(axis), *shard.shape))
    return lax.all_to_all(copies, axis, split_axis=0, concat_axis=0, tiled=True)


def joined_along(blocks, dim):
    shape = list(blocks.shape[1:])
    shape[dim] *= blocks.shape[0]
    return jnp.moveaxis(blocks, 0, dim).reshape(shape)


def gather_directly(shard, axis, dim):
    blocks = sent_to_all(shard, axis)
    return joined_along(blocks, dim)


def body(weight_gate, low_gate, high_gate, weight_up, low_up, high_up, norm_train, norm_step):
    result_gate = weight_gate.astype(jnp.float32) + mix_rate * jnp.dot(
        low_gate, high_gate, preferred_element_type=jnp.float32
    )
    result_up = weight_up.astype(jnp.float32) + mix_rate * jnp.dot(
        low_up, high_up, preferred_element_type=jnp.float32
    )
    narrow_gate, narrow_up = (result_gate.astype(jnp.bfloat16), result_up.astype(jnp.bfloat16))
    final_gate, final_up = (
        lax.all_gather(narrow_gate, "fsdp", axis=0, tiled=True),
        lax.all_gather(narrow_up, "fsdp", axis=0, tiled=True),
    )
    final_gate, final_up = (final_gate.T, final_up.T)
    serve_norm = gather_directly(
        (norm_train + norm_step).astype(jnp.bfloat16), ("fsdp", "model"), 0
    )
    return (final_gate, final_up, serve_norm)


def solution(mesh):
    return jax.shard_map(
        body,
        mesh=mesh,
        in_specs=(
            P(("ens", "fsdp"), "model"),
            P(("ens", "fsdp"), None),
            P("ens", "model"),
            P(("ens", "fsdp"), "model"),
            P(("ens", "fsdp"), None),
            P("ens", "model"),
            P(("ens", "fsdp", "model")),
            P(("ens", "fsdp", "model")),
        ),
        out_specs=(P(("ens", "model"), None), P(("ens", "model"), None), P("ens")),
        check_vma=False,
    )
```

profile of v0, /device:TPU:1, one launch (start us, length us, event | category | flops | bytes accessed | tf_op | source)
XLA Modules:
  0.0 146.5 jit_solution(759625118744581745)
XLA Ops:
  7.2 0.0 copy-start
  7.2 0.0 all-gather.3.cloned.1.call-start
  7.2 0.8 copy-done
  8.1 2.2 %fusion.3 = bf16[128,2048]{1,0:T(8,128)(2,1)} fusion(bf16[128,32]{0,1:T(8,128)(2,1)} %param.9, bf16[32,2048]{1,0:T(8,128)(2,1)S(1)} %copy-done, bf16[128,2048]{1,0:T(8,128)(2,1)} %param.8), kind=kOutput, calls=%fused_computation.5 | convolution fusion | flops 17825792 | bytes 1187840 | tf_op jit(solution)/shard_map/dot_general | solution.py:26
  10.2 0.0 all-gather.3.cloned.1.call-update
  10.3 0.0 all-gather.5.cloned.1.call-start
  10.3 2.2 %fusion.2 = bf16[128,2048]{1,0:T(8,128)(2,1)} fusion(bf16[128,32]{0,1:T(8,128)(2,1)} %param.12, bf16[32,2048]{1,0:T(8,128)(2,1)} %param.13, bf16[128,2048]{1,0:T(8,128)(2,1)} %param.11), kind=kOutput, calls=%fused_computation.4 | convolution fusion | flops 17825792 | bytes 1187840 | tf_op jit(solution)/shard_map/dot_general | solution.py:29
  12.6 0.0 all-gather.5.cloned.1.call-update
  12.6 0.7 add_convert_fusion
  13.3 22.0 %all_to_all.6 = bf16[64,1,32]{2,1,0:T(2,128)(2,1)S(1)} all-to-all(bf16[64,1,32]{2,1,0:T(2,128)(2,1)S(1)} %broadcast_in_dim.3), channel_id=1, replica_groups=mesh['ens'=4,'fsdp'=16,'model'=4] {'fsdp','model'}, dimensions={0} | all-to-all | bytes 8192 | tf_op jit(solution)/shard_map/all_to_all | solution.py:11
  35.3 0.1 reduce
  35.4 0.7 reshape.14
  36.1 35.1 %all-gather.3.cloned.1.call-done = bf16[2048,2048]{1,0:T(8,128)(2,1)} async-done(((bf16[128,2048]{1,0:T(8,128)(2,1)}), bf16[2048,2048]{1,0:T(8,128)(2,1)}) %all-gather.3.cloned.1.call-update) | async-done | bytes 8388624 | tf_op jit(solution)/shard_map/all_gather | solution.py:34
  71.2 12.2 %copy.15 = bf16[2048,2048]{1,0:T(8,128)(2,1)} copy(bf16[2048,2048]{0,1:T(8,128)(2,1)} %bitcast.6) | data formatting | bytes 16777216
  83.4 44.0 %all-gather.5.cloned.1.call-done = bf16[2048,2048]{1,0:T(8,128)(2,1)} async-done(((bf16[128,2048]{1,0:T(8,128)(2,1)}), bf16[2048,2048]{1,0:T(8,128)(2,1)}) %all-gather.5.cloned.1.call-update) | async-done | bytes 8388624 | tf_op jit(solution)/shard_map/all_gather | solution.py:35
  127.4 12.2 %copy.16 = bf16[2048,2048]{1,0:T(8,128)(2,1)} copy(bf16[2048,2048]{0,1:T(8,128)(2,1)} %bitcast.7) | data formatting | bytes 16777216
  (1 shorter events, 0.0 us)
Async XLA Ops:
  7.2 0.9 copy-start
  7.2 64.0 %all-gather.3.cloned.1.call-start = ((), (), s32[]{:S(2)}) async-start(), calls=%async_computation.1 | async-start | bytes 8912896 | tf_op jit(solution)/shard_map/all_gather | solution.py:34
  10.3 117.2 %all-gather.5.cloned.1.call-start = ((), (), s32[]{:S(2)}) async-start(), calls=%async_computation.2 | async-start | bytes 8912896 | tf_op jit(solution)/shard_map/all_gather | solution.py:35
Sparse Core Ops, SparseCore 0:
  10.4 60.7 all-gather.2
  73.0 54.3 all-gather.4
where the time goes:
time: 147 us; the launch traced here: 146 us
  waiting for transfers between devices  79.1 us (54%)
  local copies, waits for them, and re-layouts  26 us (18%)
  blocking collectives  22 us (15%)
  between operations  14.1 us (10%)
  matrix products  4.42 us (3%)
    all_gather x1, waiting for transfers between devices, body(): lax.all_gather(narrow_up, 'fsdp', axis=0, tiled=True)  44 us
    all_gather x1, waiting for transfers between devices, body(): lax.all_gather(narrow_gate, 'fsdp', axis=0, tiled=True)  35.1 us
    unnamed x4, local copies, waits for them, and re-layouts  25.3 us
    all_to_all x1, blocking collectives, sent_to_all(): return lax.all_to_all(copies, axis, split_axis=0, concat_axis=0, tiled=True)  22 us
  transfers between devices with their start and end apart: 2, of which 2 were waited for; matrix products, arithmetic and copies ran while one was open for 11% of the time, Pallas kernels for 0%

commit v1 on v0

v1 whole, which is shorter than its diff:
```python
import functools

import jax
import jax.numpy as jnp
from jax import lax
from jax.experimental import pallas as pl
from jax.experimental.pallas import tpu as pltpu
from jax.sharding import PartitionSpec as P

mix_rate = 2.0
MESH = pl.DeviceIdType.MESH
UP, DOWN = 0, 1
GATE, RISE, NORM = 0, 1, 2
LANES = 128
PIECES = 4
HOPS = {UP: (4, 3, 4), DOWN: (3, 4, 3)}
ORDER = (
    [(GATE, 0), (GATE, 1), (NORM, 0)]
    + [(GATE, p) for p in range(2, PIECES)]
    + [(RISE, p) for p in range(PIECES)]
)
PLACE = {piece: i for i, piece in enumerate(ORDER)}


def gather_kernel(
    chips, wg, lg, hg, wu, lu, hu, nt, ns, og, ou, nb,
    wv, lv, hv, ntv, nsv, xb, in_sem, send_sem, recv_sem, sib_sem, x_sem,
):
    f = lax.axis_index("fsdp")
    m = lax.axis_index("model")
    models = lax.axis_size("model")
    z, core = f // 2, f % 2
    to = {
        UP: lax.rem(z + 1, chips) * 2 + core,
        DOWN: lax.rem(z + chips - 1, chips) * 2 + core,
    }
    sibling = z * 2 + (1 - core)
    width = wg.shape[1]
    rows = width // PIECES

    loads = []
    for k, (src, dst) in enumerate(
        (
            (lg, lv.at[0]), (hg, hv.at[0]), (wg, wv.at[0]),
            (lu, lv.at[1]), (hu, hv.at[1]), (wu, wv.at[1]),
            (nt, ntv), (ns, nsv),
        )
    ):
        load = pltpu.make_async_copy(src, dst, in_sem.at[k])
        load.start()
        loads.append(load)

    barrier = pltpu.get_barrier_semaphore()
    for peer in (to[UP], to[DOWN], sibling):
        pl.semaphore_signal(
            barrier, inc=1, device_id={"fsdp": peer}, device_id_type=MESH
        )
    for k in range(1, models):
        pl.semaphore_signal(
            barrier, inc=1, device_id={"model": lax.rem(m + k, models)}, device_id_type=MESH
        )

    def piece_of(kind, p, owner):
        if kind == NORM:
            return nb.at[pl.ds(owner, 1)]
        out = og if kind == GATE else ou
        lanes = pl.ds(pl.multiple_of(owner * LANES, LANES), LANES)
        return out.at[pl.ds(p * rows, rows), lanes]

    def push(kind, p, owner):
        ref = piece_of(kind, p, owner)
        pltpu.make_async_remote_copy(
            src_ref=ref, dst_ref=ref, send_sem=send_sem.at[2, kind], recv_sem=sib_sem.at[kind],
            device_id={"fsdp": sibling}, device_id_type=MESH,
        ).start()

    def hop(way, step, kind, p, owner):
        ref = piece_of(kind, p, owner)
        return pltpu.make_async_remote_copy(
            src_ref=ref, dst_ref=ref, send_sem=send_sem.at[way, kind],
            recv_sem=recv_sem.at[way, step - 1, PLACE[kind, p]],
            device_id={"fsdp": to[way]}, device_id_type=MESH,
        )

    def send_own(kind, p):
        for way in (UP, DOWN):
            hop(way, 1, kind, p, f).start()
        push(kind, p, f)

    def merge(kind, p):
        columns = pl.ds(p * rows, rows)
        low_high = lax.dot_general(
            lv[kind], hv[kind, :, columns], (((0,), (0,)), ((), ())),
            preferred_element_type=jnp.float32,
        )
        result = wv[kind, :, columns].astype(jnp.float32) + mix_rate * low_high
        piece_of(kind, p, f)[...] = result.T.astype(jnp.bfloat16)

    for k in range(3):
        loads[k].wait()
    merge(GATE, 0)
    loads[6].wait()
    loads[7].wait()
    xb[m] = jnp.zeros((1, LANES), jnp.float32)
    xb[m, :, pl.ds(0, nt.shape[0])] = (ntv[...] + nsv[...]).reshape(1, nt.shape[0])
    merge(GATE, 1)
    pl.semaphore_wait(barrier, 3 + models - 1)
    x_copies = []
    for k in range(1, models):
        copy = pltpu.make_async_remote_copy(
            src_ref=xb.at[m], dst_ref=xb.at[m], send_sem=x_sem.at[0], recv_sem=x_sem.at[1],
            device_id={"model": lax.rem(m + k, models)}, device_id_type=MESH,
        )
        copy.start()
    send_own(GATE, 0)
    send_own(GATE, 1)
    merge(GATE, 2)
    merge(GATE, 3)
    for k in range(3, 6):
        loads[k].wait()
    merge(RISE, 0)
    others = xb.at[pl.ds(0, models - 1)]
    pltpu.make_async_copy(others, others, x_sem.at[1]).wait()
    lane = lax.broadcasted_iota(jnp.int32, (1, LANES), 1)
    part = LANES // models
    row = xb[0]
    for k in range(1, models):
        row = jnp.where(lane >= k * part, pltpu.roll(xb[k], k * part, 1), row)
    nb[f] = row
    merge(RISE, 1)
    send_own(NORM, 0)
    send_own(GATE, 2)
    send_own(GATE, 3)
    send_own(RISE, 0)
    merge(RISE, 2)
    send_own(RISE, 1)
    merge(RISE, 3)
    send_own(RISE, 2)
    pltpu.make_async_copy(others, others, x_sem.at[0]).wait()
    send_own(RISE, 3)

    arrivals = {
        way: [
            (step, kind, p)
            for step in range(1, 5)
            for kind, p in ORDER
            if step <= HOPS[way][kind]
        ]
        for way in (UP, DOWN)
    }
    for i in range(max(len(a) for a in arrivals.values())):
        for way in (UP, DOWN):
            if i >= len(arrivals[way]):
                continue
            step, kind, p = arrivals[way][i]
            back = chips - step if way == UP else step
            owner = lax.rem(z + back, chips) * 2 + core
            hop(way, step, kind, p, owner).wait_recv()
            if step < HOPS[way][kind]:
                hop(way, step + 1, kind, p, owner).start()
            push(kind, p, owner)

    for kind, out in ((NORM, nb), (GATE, og), (RISE, ou)):
        unit = out.shape[0] // (2 * chips)
        for sem, blocks in (
            (sib_sem.at[kind], chips),
            (send_sem.at[UP, kind], HOPS[UP][kind]),
            (send_sem.at[DOWN, kind], HOPS[DOWN][kind]),
            (send_sem.at[2, kind], chips),
        ):
            ref = out.at[pl.ds(0, unit * blocks)]
            pltpu.make_async_copy(ref, ref, sem).wait()


def write_kernel(og, ou, nb, fg, fu, fn, sem):
    copies = []
    cuts = 4
    for k, (src, dst) in enumerate(((og, fg), (ou, fu))):
        rows = src.shape[0] // cuts
        for c in range(cuts):
            cut = pl.ds(c * rows, rows)
            copy = pltpu.make_async_copy(src.at[cut], dst.at[cut], sem.at[k * cuts + c])
            copy.start()
            copies.append(copy)
    fn[...] = nb[...].reshape(fn.shape).astype(fn.dtype)
    for copy in copies:
        copy.wait()


def solution(mesh):
    fsdp = mesh.shape["fsdp"]
    models = mesh.shape["model"]
    chips = fsdp // 2

    def body(wg, lg, hg, wu, lu, hu, nt, ns):
        depth, width = wg.shape
        rank = lg.shape[1]
        model_width = depth * fsdp
        anywhere = pl.BlockSpec(memory_space=pl.ANY)
        on_chip = pl.BlockSpec(memory_space=pltpu.VMEM)
        og, ou, nb = pl.pallas_call(
            functools.partial(gather_kernel, chips),
            out_shape=(
                pltpu.VMEM((width, model_width), jnp.bfloat16),
                pltpu.VMEM((width, model_width), jnp.bfloat16),
                pltpu.VMEM((fsdp, 1, LANES), jnp.float32),
            ),
            in_specs=[pl.BlockSpec(memory_space=pltpu.HBM)] * 8,
            out_specs=(on_chip,) * 3,
            scratch_shapes=[
                pltpu.VMEM((2, depth, width), jnp.bfloat16),
                pltpu.VMEM((2, rank, depth), jnp.bfloat16),
                pltpu.VMEM((2, rank, width), jnp.bfloat16),
                pltpu.VMEM(nt.shape, jnp.float32),
                pltpu.VMEM(ns.shape, jnp.float32),
                pltpu.VMEM((models, 1, LANES), jnp.float32),
                pltpu.SemaphoreType.DMA((8,)),
                pltpu.SemaphoreType.DMA((3, 3)),
                pltpu.SemaphoreType.DMA((2, 4, len(ORDER))),
                pltpu.SemaphoreType.DMA((3,)),
                pltpu.SemaphoreType.DMA((2,)),
            ],
            compiler_params=pltpu.CompilerParams(
                collective_id=0, has_side_effects=True, vmem_limit_bytes=50257920
            ),
            name="gather",
        )(wg, lg.T, hg, wu, lu.T, hu, nt, ns)
        fg, fu, fn = pl.pallas_call(
            write_kernel,
            out_shape=(
                jax.ShapeDtypeStruct((width, model_width), jnp.bfloat16),
                jax.ShapeDtypeStruct((width, model_width), jnp.bfloat16),
                jax.ShapeDtypeStruct((fsdp, LANES), jnp.bfloat16),
            ),
            in_specs=[on_chip] * 3,
            out_specs=(anywhere, anywhere, on_chip),
            scratch_shapes=[pltpu.SemaphoreType.DMA((8,))],
            compiler_params=pltpu.CompilerParams(vmem_limit_bytes=20 << 20),
            name="write",
        )(og, ou, nb)
        return fg, fu, fn.reshape(fsdp * LANES)

    return jax.shard_map(
        body,
        mesh=mesh,
        in_specs=(
            P(("ens", "fsdp"), "model"),
            P(("ens", "fsdp"), None),
            P("ens", "model"),
            P(("ens", "fsdp"), "model"),
            P(("ens", "fsdp"), None),
            P("ens", "model"),
            P(("ens", "fsdp", "model")),
            P(("ens", "fsdp", "model")),
        ),
        out_specs=(P(("ens", "model"), None), P(("ens", "model"), None), P("ens")),
        check_vma=False,
    )
```

time: 147 us -> 98.7 us (0.67)
  Pallas kernels: 0 us -> 97.9 us
  waiting for transfers between devices: 79.1 us -> 0 us
  local copies, waits for them, and re-layouts: 26 us -> 0 us
  blocking collectives: 22 us -> 0 us
  between operations: 14.1 us -> 0.64 us
  matrix products: 4.42 us -> 0 us
    pallas_call x0 -> x2, Pallas kernels: none -> 97.9 us  [the longest x1 91.4 us: body(): pl.pallas_call(functools.partial(gather_kernel, chips), out_shape=(pltpu....]
    all_gather x2 -> x0, waiting for transfers between devices: 79.1 us -> none  [the longest x1 44 us: body(): lax.all_gather(narrow_up, 'fsdp', axis=0, tiled=True)]
    unnamed x4 -> x0, local copies, waits for them, and re-layouts: 25.3 us -> none
    all_to_all x1 -> x0, blocking collectives: 22 us -> none  [sent_to_all(): return lax.all_to_all(copies, axis, split_axis=0, concat_axis=0, tiled=True)]
    dot_general x2 -> x0, matrix products: 4.42 us -> none  [the longest x1 2.25 us: body(): jnp.dot(low_up, high_up, preferred_element_type=jnp.float32)]
  transfers between devices with their start and end apart: 2 -> 0, of which waited for: 2 -> 0; matrix products, arithmetic and copies ran while one was open for 11% -> 0% of each run, Pallas kernels for 0% -> 0%
where the time goes in v1:
time: 98.7 us; the launch traced here: 98.5 us
  Pallas kernels  97.9 us (99%)
    pallas_call x1, Pallas kernels, body(): pl.pallas_call(functools.partial(gather_kernel, chips), out_shape=(pltpu....  91.4 us
    pallas_call x1, Pallas kernels, body(): pl.pallas_call(write_kernel, out_shape=(jax.ShapeDtypeStruct((width, mode...  6.52 us

profile of v1, /device:TPU:1, one launch (start us, length us, event | category | flops | bytes accessed | tf_op | source)
XLA Modules:
  0.0 98.5 jit_solution(5615097720718231023)
XLA Ops:
  0.6 91.4 %gather.1 = (bf16[2048,2048]{1,0:T(8,128)(2,1)S(1)}, bf16[2048,2048]{1,0:T(8,128)(2,1)S(1)}, f32[16,1,128]{2,1,0:T(1,128)S(1)}) custom-call(bf16[128,2048]{1,0:T(8,128)(2,1)} %wg.1, bf16[32,128]{1,0:T(8,128)(2,1)} %bitcast.3, bf16[32,2048]{1,0:T(8,128)(2,1)} %hg.1, bf16[128,2048]{1,0:T(8,128)(2,1)} %wu.1, bf16[32,128]{1,0:T(8,128)(2,1)} %bitcast.4, ...), custom_call_target="tpu_custom_call" | custom-call | tf_op jit(solution)/shard_map/gather/pallas_call | solution.py:201
  92.0 6.5 %write.1 = (bf16[2048,2048]{1,0:T(8,128)(2,1)}, bf16[2048,2048]{1,0:T(8,128)(2,1)}, bf16[16,128]{1,0:T(8,128)(2,1)}) custom-call(bf16[2048,2048]{1,0:T(8,128)(2,1)S(1)} %get-tuple-element.9.og, bf16[2048,2048]{1,0:T(8,128)(2,1)S(1)} %get-tuple-element.10.ou, f32[16,1,128]{2,1,0:T(1,128)S(1)} %get-tuple-element.11.nb), custom_call_target="tpu_custom_call" | custom-call | tf_op jit(solution)/shard_map/write/pallas_call | solution.py:228

commit v2 on v1

--- a/solution.py
+++ b/solution.py
@@ -12,13 +12,10 @@
 UP, DOWN = 0, 1
 GATE, RISE, NORM = 0, 1, 2
 LANES = 128
-PIECES = 4
+CUTS = {GATE: (256, 512, 512, 512, 128, 128), RISE: (512, 512, 512, 256, 128, 128), NORM: (1,)}
 HOPS = {UP: (4, 3, 4), DOWN: (3, 4, 3)}
-ORDER = (
-    [(GATE, 0), (GATE, 1), (NORM, 0)]
-    + [(GATE, p) for p in range(2, PIECES)]
-    + [(RISE, p) for p in range(PIECES)]
-)
+ORDER = [(GATE, p) for p in range(len(CUTS[GATE]))] + [(RISE, p) for p in range(len(CUTS[RISE]))]
+ORDER.insert(3, (NORM, 0))
 PLACE = {piece: i for i, piece in enumerate(ORDER)}
 
 
@@ -35,8 +32,6 @@
         DOWN: lax.rem(z + chips - 1, chips) * 2 + core,
     }
     sibling = z * 2 + (1 - core)
-    width = wg.shape[1]
-    rows = width // PIECES
 
     loads = []
     for k, (src, dst) in enumerate(
@@ -60,12 +55,15 @@
             barrier, inc=1, device_id={"model": lax.rem(m + k, models)}, device_id_type=MESH
         )
 
+    def rows_of(kind, p):
+        return pl.ds(sum(CUTS[kind][:p]), CUTS[kind][p])
+
     def piece_of(kind, p, owner):
         if kind == NORM:
             return nb.at[pl.ds(owner, 1)]
         out = og if kind == GATE else ou
         lanes = pl.ds(pl.multiple_of(owner * LANES, LANES), LANES)
-        return out.at[pl.ds(p * rows, rows), lanes]
+        return out.at[rows_of(kind, p), lanes]
 
     def push(kind, p, owner):
         ref = piece_of(kind, p, owner)
@@ -88,7 +86,7 @@
         push(kind, p, f)
 
     def merge(kind, p):
-        columns = pl.ds(p * rows, rows)
+        columns = rows_of(kind, p)
         low_high = lax.dot_general(
             lv[kind], hv[kind, :, columns], (((0,), (0,)), ((), ())),
             preferred_element_type=jnp.float32,
@@ -96,48 +94,56 @@
         result = wv[kind, :, columns].astype(jnp.float32) + mix_rate * low_high
         piece_of(kind, p, f)[...] = result.T.astype(jnp.bfloat16)
 
+    others = xb.at[pl.ds(0, models - 1)]
+    lane = lax.broadcasted_iota(jnp.int32, (1, LANES), 1)
+    part = LANES // models
+
+    def norm_part():
+        loads[6].wait()
+        loads[7].wait()
+        xb[m] = jnp.zeros((1, LANES), jnp.float32)
+        xb[m, :, pl.ds(0, part)] = (ntv[...] + nsv[...]).reshape(1, part)
+
+    def norm_exchange():
+        for k in range(1, models):
+            pltpu.make_async_remote_copy(
+                src_ref=xb.at[m], dst_ref=xb.at[m], send_sem=x_sem.at[0], recv_sem=x_sem.at[1],
+                device_id={"model": lax.rem(m + k, models)}, device_id_type=MESH,
+            ).start()
+
+    def norm_row():
+        pltpu.make_async_copy(others, others, x_sem.at[1]).wait()
+        row = xb[0]
+        for k in range(1, models):
+            row = jnp.where(lane >= k * part, pltpu.roll(xb[k], k * part, 1), row)
+        nb[f] = row
+
     for k in range(3):
         loads[k].wait()
     merge(GATE, 0)
-    loads[6].wait()
-    loads[7].wait()
-    xb[m] = jnp.zeros((1, LANES), jnp.float32)
-    xb[m, :, pl.ds(0, nt.shape[0])] = (ntv[...] + nsv[...]).reshape(1, nt.shape[0])
-    merge(GATE, 1)
+    norm_part()
     pl.semaphore_wait(barrier, 3 + models - 1)
-    x_copies = []
-    for k in range(1, models):
-        copy = pltpu.make_async_remote_copy(
-            src_ref=xb.at[m], dst_ref=xb.at[m], send_sem=x_sem.at[0], recv_sem=x_sem.at[1],
-            device_id={"model": lax.rem(m + k, models)}, device_id_type=MESH,
-        )
-        copy.start()
     send_own(GATE, 0)
-    send_own(GATE, 1)
-    merge(GATE, 2)
-    merge(GATE, 3)
-    for k in range(3, 6):
-        loads[k].wait()
-    merge(RISE, 0)
-    others = xb.at[pl.ds(0, models - 1)]
-    pltpu.make_async_copy(others, others, x_sem.at[1]).wait()
-    lane = lax.broadcasted_iota(jnp.int32, (1, LANES), 1)
-    part = LANES // models
-    row = xb[0]
-    for k in range(1, models):
-        row = jnp.where(lane >= k * part, pltpu.roll(xb[k], k * part, 1), row)
-    nb[f] = row
-    merge(RISE, 1)
-    send_own(NORM, 0)
-    send_own(GATE, 2)
-    send_own(GATE, 3)
-    send_own(RISE, 0)
-    merge(RISE, 2)
-    send_own(RISE, 1)
-    merge(RISE, 3)
-    send_own(RISE, 2)
+    norm_exchange()
+    made = [piece for piece in ORDER if piece[0] != NORM]
+    pending = []
+    for i, piece in enumerate(made[1:]):
+        if piece == (RISE, 0):
+            for k in range(3, 6):
+                loads[k].wait()
+            norm_row()
+            pending.insert(0, (NORM, 0))
+        merge(*piece)
+        pending.append(piece)
+        if piece[0] == GATE and piece[1] < 3:
+            if len(pending) > 1:
+                send_own(*pending.pop(0))
+        elif piece[0] == RISE:
+            while len(pending) > 1:
+                send_own(*pending.pop(0))
     pltpu.make_async_copy(others, others, x_sem.at[0]).wait()
-    send_own(RISE, 3)
+    while pending:
+        send_own(*pending.pop(0))
 
     arrivals = {
         way: [
@@ -172,17 +178,18 @@
             pltpu.make_async_copy(ref, ref, sem).wait()
 
 
-def write_kernel(og, ou, nb, fg, fu, fn, sem):
+def write_kernel(og, ou, nb, fg, fu, fn, norm, sem):
+    norm[...] = nb[...].reshape(norm.shape).astype(norm.dtype)
     copies = []
     cuts = 4
     for k, (src, dst) in enumerate(((og, fg), (ou, fu))):
         rows = src.shape[0] // cuts
         for c in range(cuts):
             cut = pl.ds(c * rows, rows)
-            copy = pltpu.make_async_copy(src.at[cut], dst.at[cut], sem.at[k * cuts + c])
-            copy.start()
-            copies.append(copy)
-    fn[...] = nb[...].reshape(fn.shape).astype(fn.dtype)
+            copies.append(pltpu.make_async_copy(src.at[cut], dst.at[cut], sem.at[k * cuts + c]))
+            copies[-1].start()
+    copies.append(pltpu.make_async_copy(norm, fn, sem.at[2 * cuts]))
+    copies[-1].start()
     for copy in copies:
         copy.wait()
 
@@ -233,8 +240,8 @@
                 jax.ShapeDtypeStruct((fsdp, LANES), jnp.bfloat16),
             ),
             in_specs=[on_chip] * 3,
-            out_specs=(anywhere, anywhere, on_chip),
-            scratch_shapes=[pltpu.SemaphoreType.DMA((8,))],
+            out_specs=(anywhere,) * 3,
+            scratch_shapes=[pltpu.VMEM((fsdp, LANES), jnp.bfloat16), pltpu.SemaphoreType.DMA((9,))],
             compiler_params=pltpu.CompilerParams(vmem_limit_bytes=20 << 20),
             name="write",
         )(og, ou, nb)

time: 98.7 us -> 98.2 us (level)
  no operation moved by 1% of the time
where the time goes in v2:
time: 98.2 us; the launch traced here: 98.1 us
  Pallas kernels  97.4 us (99%)
    pallas_call x1, Pallas kernels, body(): pl.pallas_call(functools.partial(gather_kernel, chips), out_shape=(pltpu....  91.5 us
    pallas_call x1, Pallas kernels, body(): pl.pallas_call(write_kernel, out_shape=(jax.ShapeDtypeStruct((width, mode...  5.94 us

profile of v2, /device:TPU:1, one launch (start us, length us, event | category | flops | bytes accessed | tf_op | source)
XLA Modules:
  0.0 98.1 jit_solution(5938562402838912927)
XLA Ops:
  0.6 91.5 %gather.1 = (bf16[2048,2048]{1,0:T(8,128)(2,1)S(1)}, bf16[2048,2048]{1,0:T(8,128)(2,1)S(1)}, f32[16,1,128]{2,1,0:T(1,128)S(1)}) custom-call(bf16[128,2048]{1,0:T(8,128)(2,1)} %wg.1, bf16[32,128]{1,0:T(8,128)(2,1)} %bitcast.3, bf16[32,2048]{1,0:T(8,128)(2,1)} %hg.1, bf16[128,2048]{1,0:T(8,128)(2,1)} %wu.1, bf16[32,128]{1,0:T(8,128)(2,1)} %bitcast.4, ...), custom_call_target="tpu_custom_call" | custom-call | tf_op jit(solution)/shard_map/gather/pallas_call | solution.py:208
  92.2 5.9 %write.1 = (bf16[2048,2048]{1,0:T(8,128)(2,1)}, bf16[2048,2048]{1,0:T(8,128)(2,1)}, bf16[16,128]{1,0:T(8,128)(2,1)}) custom-call(bf16[2048,2048]{1,0:T(8,128)(2,1)S(1)} %get-tuple-element.9.og, bf16[2048,2048]{1,0:T(8,128)(2,1)S(1)} %get-tuple-element.10.ou, f32[16,1,128]{2,1,0:T(1,128)S(1)} %get-tuple-element.11.nb), custom_call_target="tpu_custom_call" | custom-call | tf_op jit(solution)/shard_map/write/pallas_call | solution.py:235

commit v3 on v2

v3 whole, which is shorter than its diff:
```python
import functools

import jax
import jax.numpy as jnp
from jax import lax
from jax.experimental import pallas as pl
from jax.experimental.pallas import tpu as pltpu
from jax.sharding import PartitionSpec as P

mix_rate = 2.0
MESH = pl.DeviceIdType.MESH
UP, DOWN = 0, 1
GATE, RISE, NORM = 0, 1, 2
LANES = 128
CUTS = {GATE: (256, 512, 512, 512, 128, 128), RISE: (512, 512, 512, 256, 128, 128), NORM: (1,)}
HOPS = {UP: (4, 3, 4), DOWN: (3, 4, 3)}
ORDER = [(GATE, p) for p in range(len(CUTS[GATE]))] + [(RISE, p) for p in range(len(CUTS[RISE]))]
ORDER.insert(3, (NORM, 0))
ARRIVALS = {
    way: [
        (step, kind, p)
        for step in range(1, 5)
        for kind, p in ORDER
        if step <= HOPS[way][kind]
    ]
    for way in (UP, DOWN)
}
FIRST = (27, 41)
LEAST = min(FIRST)
AHEAD = FIRST.index(LEAST)
MEET = 36


def early(core, way, step, kind, p):
    return ARRIVALS[way].index((step, kind, p)) < FIRST[core]


def shared_early(way, i):
    return i < LEAST


def position(chips):
    f = lax.axis_index("fsdp")
    z, core = f // 2, f % 2
    to = {
        UP: lax.rem(z + 1, chips) * 2 + core,
        DOWN: lax.rem(z + chips - 1, chips) * 2 + core,
    }
    return f, z, core, to, z * 2 + (1 - core)


def owner_of(chips, z, core, way, step):
    back = chips - step if way == UP else step
    return lax.rem(z + back, chips) * 2 + core


def rows_of(kind, p):
    return pl.ds(sum(CUTS[kind][:p]), CUTS[kind][p])


def lanes_of(owner):
    return pl.ds(pl.multiple_of(owner * LANES, LANES), LANES)


def piece_of(held, kind, p, owner):
    if kind == NORM:
        return held[NORM].at[pl.ds(owner, 1)]
    return held[kind].at[rows_of(kind, p), lanes_of(owner)]


def copy_to(source, target, send_sem, recv_sem, fsdp):
    return pltpu.make_async_remote_copy(
        src_ref=source, dst_ref=target, send_sem=send_sem, recv_sem=recv_sem,
        device_id={"fsdp": fsdp}, device_id_type=MESH,
    )


def wait_for(held, kind, rows, sem):
    if rows:
        ref = held[kind].at[pl.ds(0, rows if kind == NORM else rows * LANES // held[kind].shape[1])]
        pltpu.make_async_copy(ref, ref, sem).wait()


def rows_in(pieces):
    return [sum(CUTS[k][p] for k, p in pieces if k == kind) for kind in (GATE, RISE, NORM)]


def each(first, last):
    for i in range(first, last):
        for way in (UP, DOWN):
            if i < len(ARRIVALS[way]):
                yield i, way, *ARRIVALS[way][i]


COUNT = max(len(a) for a in ARRIVALS.values())


def gather_kernel(
    chips, wg, lg, hg, wu, lu, hu, nt, ns, og, ou, nb,
    wv, lv, hv, ntv, nsv, xb, in_sem, send_sem, recv_sem, sib_sem, x_sem,
):
    f, z, core, to, sibling = position(chips)
    m = lax.axis_index("model")
    models = lax.axis_size("model")
    held = (og, ou, nb)

    loads = []
    for k, (src, dst) in enumerate(
        (
            (lg, lv.at[0]), (hg, hv.at[0]), (wg, wv.at[0]),
            (lu, lv.at[1]), (hu, hv.at[1]), (wu, wv.at[1]),
            (nt, ntv), (ns, nsv),
        )
    ):
        load = pltpu.make_async_copy(src, dst, in_sem.at[k])
        load.start()
        loads.append(load)

    barrier = pltpu.get_barrier_semaphore()
    for peer in (to[UP], to[DOWN], sibling):
        pl.semaphore_signal(
            barrier, inc=1, device_id={"fsdp": peer}, device_id_type=MESH
        )
    for k in range(1, models):
        pl.semaphore_signal(
            barrier, inc=1, device_id={"model": lax.rem(m + k, models)}, device_id_type=MESH
        )

    def push(kind, p, owner):
        ref = piece_of(held, kind, p, owner)
        copy_to(ref, ref, send_sem.at[2, kind], sib_sem.at[kind], sibling).start()

    def hop(way, step, kind, p, owner):
        ref = piece_of(held, kind, p, owner)
        place = ARRIVALS[way].index((step, kind, p))
        return copy_to(ref, ref, send_sem.at[way, kind], recv_sem.at[way, place], to[way])

    def send_own(kind, p):
        for way in (UP, DOWN):
            hop(way, 1, kind, p, f).start()
        push(kind, p, f)

    def merge(kind, p):
        columns = rows_of(kind, p)
        low_high = lax.dot_general(
            lv[kind], hv[kind, :, columns], (((0,), (0,)), ((), ())),
            preferred_element_type=jnp.float32,
        )
        result = wv[kind, :, columns].astype(jnp.float32) + mix_rate * low_high
        piece_of(held, kind, p, f)[...] = result.T.astype(jnp.bfloat16)

    others = xb.at[pl.ds(0, models - 1)]
    lane = lax.broadcasted_iota(jnp.int32, (1, LANES), 1)
    part = LANES // models

    def norm_part():
        loads[6].wait()
        loads[7].wait()
        xb[m] = jnp.zeros((1, LANES), jnp.float32)
        xb[m, :, pl.ds(0, part)] = (ntv[...] + nsv[...]).reshape(1, part)

    def norm_exchange():
        for k in range(1, models):
            pltpu.make_async_remote_copy(
                src_ref=xb.at[m], dst_ref=xb.at[m], send_sem=x_sem.at[0], recv_sem=x_sem.at[1],
                device_id={"model": lax.rem(m + k, models)}, device_id_type=MESH,
            ).start()

    def norm_row():
        pltpu.make_async_copy(others, others, x_sem.at[1]).wait()
        row = xb[0]
        for k in range(1, models):
            row = jnp.where(lane >= k * part, pltpu.roll(xb[k], k * part, 1), row)
        nb[f] = row

    for k in range(3):
        loads[k].wait()
    merge(GATE, 0)
    norm_part()
    pl.semaphore_wait(barrier, 3 + models - 1)
    send_own(GATE, 0)
    norm_exchange()
    made = [piece for piece in ORDER if piece[0] != NORM]
    pending = []
    for i, piece in enumerate(made[1:]):
        if piece == (RISE, 0):
            for k in range(3, 6):
                loads[k].wait()
            norm_row()
            pending.insert(0, (NORM, 0))
        merge(*piece)
        pending.append(piece)
        if piece[0] == GATE and piece[1] < 3:
            if len(pending) > 1:
                send_own(*pending.pop(0))
        elif piece[0] == RISE:
            while len(pending) > 1:
                send_own(*pending.pop(0))
    pltpu.make_async_copy(others, others, x_sem.at[0]).wait()
    while pending:
        send_own(*pending.pop(0))

    def take(c):
        sent = {way: list(ORDER) for way in (UP, DOWN)}
        pushed = list(ORDER)
        for i, way, step, kind, p in each(0, FIRST[c]):
            owner = owner_of(chips, z, core, way, step)
            hop(way, step, kind, p, owner).wait_recv()
            if step < HOPS[way][kind] and early(c, way, step + 1, kind, p):
                hop(way, step + 1, kind, p, owner).start()
                sent[way].append((kind, p))
            if shared_early(way, i):
                push(kind, p, owner)
                pushed.append((kind, p))
        for kind in (NORM, GATE, RISE):
            for way in (UP, DOWN):
                wait_for(held, kind, rows_in(sent[way])[kind], send_sem.at[way, kind])
            wait_for(held, kind, rows_in(pushed)[kind], send_sem.at[2, kind])
            wait_for(held, kind, rows_in(pushed)[kind], sib_sem.at[kind])

    for c in (0, 1):
        pl.when(core == c)(functools.partial(take, c))


def finish_kernel(chips, og, ou, nb, after, lg, lu, ln, send_sem, recv_sem, sib_sem, ready):
    f, z, core, to, sibling = position(chips)
    before, held = (og, ou, nb), (lg, lu, ln)
    barrier = pltpu.get_barrier_semaphore()
    for peer in (to[UP], to[DOWN]):
        pl.semaphore_signal(
            barrier, inc=1, device_id={"fsdp": peer}, device_id_type=MESH
        )

    @pl.when(core == AHEAD)
    def _():
        pl.semaphore_signal(
            barrier, inc=1, device_id={"fsdp": sibling}, device_id_type=MESH
        )
        pl.semaphore_wait(barrier, 2)

    @pl.when(core != AHEAD)
    def _():
        pl.semaphore_wait(barrier, 3)
        pl.semaphore_signal(
            ready, inc=1, device_id={"fsdp": sibling}, device_id_type=MESH
        )

    def push(source, kind, p, owner):
        copy_to(
            piece_of(source, kind, p, owner), piece_of(held, kind, p, owner),
            send_sem.at[2, kind], sib_sem.at[kind], sibling,
        ).start()

    def hop(source, way, step, kind, p, owner):
        place = ARRIVALS[way].index((step, kind, p))
        return copy_to(
            piece_of(source, kind, p, owner), piece_of(held, kind, p, owner),
            send_sem.at[way, kind], recv_sem.at[way, place], to[way],
        )

    def take(c):
        sent = {way: [] for way in (UP, DOWN)}
        pushed, late = [], []
        for i, way, step, kind, p in each(0, FIRST[c]):
            owner = owner_of(chips, z, core, way, step)
            if step < HOPS[way][kind] and not early(c, way, step + 1, kind, p):
                hop(before, way, step + 1, kind, p, owner).start()
                sent[way].append((kind, p))
            if not shared_early(way, i):
                late.append((before, kind, p, way, step))

        def push_late():
            while late:
                source, kind, p, way, step = late.pop(0)
                push(source, kind, p, owner_of(chips, z, core, way, step))
                pushed.append((kind, p))

        met = c != AHEAD
        for i, way, step, kind, p in each(FIRST[c], COUNT):
            if not met and i >= MEET:
                pl.semaphore_wait(ready, 1)
                met = True
            if met:
                push_late()
            owner = owner_of(chips, z, core, way, step)
            hop(held, way, step, kind, p, owner).wait_recv()
            if step < HOPS[way][kind]:
                hop(held, way, step + 1, kind, p, owner).start()
                sent[way].append((kind, p))
            late.append((held, kind, p, way, step))
        push_late()
        coming = [(kind, p) for _, _, _, kind, p in each(LEAST, COUNT)]
        for kind in (NORM, GATE, RISE):
            for way in (UP, DOWN):
                wait_for(held, kind, rows_in(sent[way])[kind], send_sem.at[way, kind])
            wait_for(held, kind, rows_in(pushed)[kind], send_sem.at[2, kind])
            wait_for(held, kind, rows_in(coming)[kind], sib_sem.at[kind])

    for c in (0, 1):
        pl.when(core == c)(functools.partial(take, c))


def runs(pieces):
    out = []
    for kind, p in sorted(pieces):
        start, size = sum(CUTS[kind][:p]), CUTS[kind][p]
        if out and out[-1][0] == kind and sum(out[-1][1:]) == start:
            out[-1] = (kind, out[-1][1], out[-1][2] + size)
        else:
            out.append((kind, start, size))
    return out


def store(chips, z, core, c, held, final, sem, sides, own):
    total = [0, 0]
    for mine, (first, last) in ((True, sides[0]), (False, sides[1])):
        line = core if mine else 1 - core
        blocks = {}
        for _, way, step, kind, p in each(first, last):
            if kind != NORM:
                blocks.setdefault((way, step), []).append((kind, p))
        if own:
            blocks[UP, 0] = [piece for piece in ORDER if piece[0] != NORM]
        for (way, step), pieces in blocks.items():
            lanes = lanes_of(owner_of(chips, z, line, way, step))
            for kind, start, size in runs(pieces):
                at = (pl.ds(start, size), lanes)
                pltpu.make_async_copy(held[kind].at[at], final[kind].at[at], sem.at[kind]).start()
                total[kind] += size
    return total


def write_kernel(chips, og, ou, fg, fu, after, sem):
    _, z, core, _, _ = position(chips)
    after[...] = jnp.zeros_like(after)
    held, final = (og, ou), (fg, fu)

    def take(c):
        total = store(chips, z, core, c, held, final, sem, ((0, FIRST[c]), (0, LEAST)), True)
        for kind in (GATE, RISE):
            wait_for(held, kind, total[kind], sem.at[kind])

    for c in (0, 1):
        pl.when(core == c)(functools.partial(take, c))


def write_rest_kernel(chips, fg_in, fu_in, nb, lg, lu, ln, fg, fu, fn, rows, norm, sem):
    f, z, core, _, sibling = position(chips)
    held, final = (lg, lu), (fg, fu)

    def take(c):
        total = store(
            chips, z, core, c, held, final, sem, ((FIRST[c], COUNT), (LEAST, COUNT)), False
        )
        rows[f] = nb[f]
        rows[sibling] = nb[sibling]
        for i, way, step, kind, p in each(0, COUNT):
            if kind == NORM:
                for line, source in ((core, i < FIRST[c]), (1 - core, i < LEAST)):
                    owner = owner_of(chips, z, line, way, step)
                    rows[owner] = nb[owner] if source else ln[owner]
        norm[...] = rows[...].reshape(norm.shape).astype(norm.dtype)
        last = pltpu.make_async_copy(norm, fn, sem.at[2])
        last.start()
        for kind in (GATE, RISE):
            wait_for(held, kind, total[kind], sem.at[kind])
        last.wait()

    for c in (0, 1):
        pl.when(core == c)(functools.partial(take, c))


def solution(mesh):
    fsdp = mesh.shape["fsdp"]
    models = mesh.shape["model"]
    chips = fsdp // 2

    def body(wg, lg, hg, wu, lu, hu, nt, ns):
        depth, width = wg.shape
        rank = lg.shape[1]
        model_width = depth * fsdp
        anywhere = pl.BlockSpec(memory_space=pl.ANY)
        on_chip = pl.BlockSpec(memory_space=pltpu.VMEM)
        final = jax.ShapeDtypeStruct((width, model_width), jnp.bfloat16)
        on_chip_held = (
            pltpu.VMEM((width, model_width), jnp.bfloat16),
            pltpu.VMEM((width, model_width), jnp.bfloat16),
            pltpu.VMEM((fsdp, 1, LANES), jnp.float32),
        )
        ring_sems = [
            pltpu.SemaphoreType.DMA((3, 3)),
            pltpu.SemaphoreType.DMA((2, COUNT)),
            pltpu.SemaphoreType.DMA((3,)),
        ]
        og, ou, nb = pl.pallas_call(
            functools.partial(gather_kernel, chips),
            out_shape=on_chip_held,
            in_specs=[pl.BlockSpec(memory_space=pltpu.HBM)] * 8,
            out_specs=(on_chip,) * 3,
            scratch_shapes=[
                pltpu.VMEM((2, depth, width), jnp.bfloat16),
                pltpu.VMEM((2, rank, depth), jnp.bfloat16),
                pltpu.VMEM((2, rank, width), jnp.bfloat16),
                pltpu.VMEM(nt.shape, jnp.float32),
                pltpu.VMEM(ns.shape, jnp.float32),
                pltpu.VMEM((models, 1, LANES), jnp.float32),
                pltpu.SemaphoreType.DMA((8,)),
                *ring_sems,
                pltpu.SemaphoreType.DMA((2,)),
            ],
            compiler_params=pltpu.CompilerParams(
                collective_id=0, has_side_effects=True, vmem_limit_bytes=50257920
            ),
            name="gather",
        )(wg, lg.T, hg, wu, lu.T, hu, nt, ns)
        fg, fu, after = pl.pallas_call(
            functools.partial(write_kernel, chips),
            out_shape=(final, final, pltpu.VMEM((8, LANES), jnp.float32)),
            in_specs=[on_chip] * 2,
            out_specs=(anywhere, anywhere, on_chip),
            scratch_shapes=[pltpu.SemaphoreType.DMA((2,))],
            compiler_params=pltpu.CompilerParams(vmem_limit_bytes=4 << 20),
            name="write",
        )(og, ou)
        lg2, lu2, ln = pl.pallas_call(
            functools.partial(finish_kernel, chips),
            out_shape=on_chip_held,
            in_specs=[on_chip] * 4,
            out_specs=(on_chip,) * 3,
            scratch_shapes=[*ring_sems, pltpu.SemaphoreType.REGULAR],
            compiler_params=pltpu.CompilerParams(
                collective_id=1, has_side_effects=True, vmem_limit_bytes=4 << 20
            ),
            name="finish",
        )(og, ou, nb, after)
        fg, fu, fn = pl.pallas_call(
            functools.partial(write_rest_kernel, chips),
            out_shape=(final, final, jax.ShapeDtypeStruct((fsdp, LANES), jnp.bfloat16)),
            in_specs=[anywhere] * 2 + [on_chip] * 4,
            out_specs=(anywhere,) * 3,
            scratch_shapes=[
                pltpu.VMEM((fsdp, 1, LANES), jnp.float32),
                pltpu.VMEM((fsdp, LANES), jnp.bfloat16),
                pltpu.SemaphoreType.DMA((3,)),
            ],
            input_output_aliases={0: 0, 1: 1},
            compiler_params=pltpu.CompilerParams(vmem_limit_bytes=4 << 20),
            name="write_rest",
        )(fg, fu, nb, lg2, lu2, ln)
        return fg, fu, fn.reshape(fsdp * LANES)

    return jax.shard_map(
        body,
        mesh=mesh,
        in_specs=(
            P(("ens", "fsdp"), "model"),
            P(("ens", "fsdp"), None),
            P("ens", "model"),
            P(("ens", "fsdp"), "model"),
            P(("ens", "fsdp"), None),
            P("ens", "model"),
            P(("ens", "fsdp", "model")),
            P(("ens", "fsdp", "model")),
        ),
        out_specs=(P(("ens", "model"), None), P(("ens", "model"), None), P("ens")),
        check_vma=False,
    )
```

time: 98.2 us -> 94 us (0.957)
  Pallas kernels: 97.4 us -> 93.2 us
    pallas_call x2 -> x4, Pallas kernels: 97.4 us -> 93.2 us  [the longest x1 71.2 us: body(): pl.pallas_call(functools.partial(gather_kernel, chips), out_shape=on_chip...]
where the time goes in v3:
time: 94 us; the launch traced here: 93.8 us
  Pallas kernels  93.2 us (99%)
    pallas_call x1, Pallas kernels, body(): pl.pallas_call(functools.partial(gather_kernel, chips), out_shape=on_chip...  71.2 us
    pallas_call x1, Pallas kernels, body(): pl.pallas_call(functools.partial(finish_kernel, chips), out_shape=on_chip...  15.4 us
    pallas_call x1, Pallas kernels, body(): pl.pallas_call(functools.partial(write_kernel, chips), out_shape=(final,...  4.76 us

profile of v3, /device:TPU:1, one launch (start us, length us, event | category | flops | bytes accessed | tf_op | source)
XLA Modules:
  0.0 93.8 jit_solution(15565901145743198212)
XLA Ops:
  0.6 71.2 %gather.1 = (bf16[2048,2048]{1,0:T(8,128)(2,1)S(1)}, bf16[2048,2048]{1,0:T(8,128)(2,1)S(1)}, f32[16,1,128]{2,1,0:T(1,128)S(1)}) custom-call(bf16[128,2048]{1,0:T(8,128)(2,1)} %wg.1, bf16[32,128]{1,0:T(8,128)(2,1)} %bitcast.3, bf16[32,2048]{1,0:T(8,128)(2,1)} %hg.1, bf16[128,2048]{1,0:T(8,128)(2,1)} %wu.1, bf16[32,128]{1,0:T(8,128)(2,1)} %bitcast.4, ...), custom_call_target="tpu_custom_call" | custom-call | tf_op jit(solution)/shard_map/gather/pallas_call | solution.py:395
  71.8 4.8 %write.1 = (bf16[2048,2048]{1,0:T(8,128)(2,1)}, bf16[2048,2048]{1,0:T(8,128)(2,1)}, f32[8,128]{1,0:T(8,128)S(1)}) custom-call(bf16[2048,2048]{1,0:T(8,128)(2,1)S(1)} %get-tuple-element.15.og, bf16[2048,2048]{1,0:T(8,128)(2,1)S(1)} %get-tuple-element.16.ou), custom_call_target="tpu_custom_call" | custom-call | tf_op jit(solution)/shard_map/write/pallas_call | solution.py:416
  76.6 15.4 %finish.1 = (bf16[2048,2048]{1,0:T(8,128)(2,1)S(1)}, bf16[2048,2048]{1,0:T(8,128)(2,1)S(1)}, f32[16,1,128]{2,1,0:T(1,128)S(1)}) custom-call(bf16[2048,2048]{1,0:T(8,128)(2,1)S(1)} %get-tuple-element.15.og, bf16[2048,2048]{1,0:T(8,128)(2,1)S(1)} %get-tuple-element.16.ou, f32[16,1,128]{2,1,0:T(1,128)S(1)} %get-tuple-element.19.nb, ...), custom_call_target="tpu_custom_call" | custom-call | tf_op jit(solution)/shard_map/finish/pallas_call | solution.py:425
  92.0 1.9 %write_rest.1 = (bf16[2048,2048]{1,0:T(8,128)(2,1)}, bf16[2048,2048]{1,0:T(8,128)(2,1)}, bf16[16,128]{1,0:T(8,128)(2,1)}) custom-call(bf16[2048,2048]{1,0:T(8,128)(2,1)} %get-tuple-element.17.fg_in, bf16[2048,2048]{1,0:T(8,128)(2,1)} %get-tuple-element.18.fu_in, ...), custom_call_target="tpu_custom_call", output_to_operand_aliasing={{0}: (0, {}), {1}: (1, {})} | custom-call | tf_op jit(solution)/shard_map/write_rest/pallas_call | solution.py:436

commit v4 on v3

--- a/solution.py
+++ b/solution.py
@@ -12,7 +12,7 @@
 UP, DOWN = 0, 1
 GATE, RISE, NORM = 0, 1, 2
 LANES = 128
-CUTS = {GATE: (256, 512, 512, 512, 128, 128), RISE: (512, 512, 512, 256, 128, 128), NORM: (1,)}
+CUTS = {GATE: (256, 512, 512, 256, 256, 128, 128), RISE: (512, 512, 512, 256, 128, 128), NORM: (1,)}
 HOPS = {UP: (4, 3, 4), DOWN: (3, 4, 3)}
 ORDER = [(GATE, p) for p in range(len(CUTS[GATE]))] + [(RISE, p) for p in range(len(CUTS[RISE]))]
 ORDER.insert(3, (NORM, 0))
@@ -25,10 +25,10 @@
     ]
     for way in (UP, DOWN)
 }
-FIRST = (27, 41)
+FIRST = (29, 45)
 LEAST = min(FIRST)
 AHEAD = FIRST.index(LEAST)
-MEET = 36
+MEET = 39
 
 
 def early(core, way, step, kind, p):
@@ -93,29 +93,32 @@
 
 
 COUNT = max(len(a) for a in ARRIVALS.values())
+MOVED = (GATE, 4)
+
+
+def moved(way, step, kind, p):
+    return (kind, p) == MOVED and way == UP and step == 4
 
 
 def gather_kernel(
     chips, wg, lg, hg, wu, lu, hu, nt, ns, og, ou, nb,
     wv, lv, hv, ntv, nsv, xb, in_sem, send_sem, recv_sem, sib_sem, x_sem,
 ):
+    loads = []
+    for k, (src, dst) in enumerate(
+        (
+            (lg, lv.at[0]), (hg, hv.at[0]), (wg, wv.at[0]), (nt, ntv), (ns, nsv),
+            (lu, lv.at[1]), (hu, hv.at[1]), (wu, wv.at[1]),
+        )
+    ):
+        load = pltpu.make_async_copy(src, dst, in_sem.at[k])
+        load.start()
+        loads.append(load)
+
     f, z, core, to, sibling = position(chips)
     m = lax.axis_index("model")
     models = lax.axis_size("model")
     held = (og, ou, nb)
-
-    loads = []
-    for k, (src, dst) in enumerate(
-        (
-            (lg, lv.at[0]), (hg, hv.at[0]), (wg, wv.at[0]),
-            (lu, lv.at[1]), (hu, hv.at[1]), (wu, wv.at[1]),
-            (nt, ntv), (ns, nsv),
-        )
-    ):
-        load = pltpu.make_async_copy(src, dst, in_sem.at[k])
-        load.start()
-        loads.append(load)
-
     barrier = pltpu.get_barrier_semaphore()
     for peer in (to[UP], to[DOWN], sibling):
         pl.semaphore_signal(
@@ -154,8 +157,8 @@
     part = LANES // models
 
     def norm_part():
-        loads[6].wait()
-        loads[7].wait()
+        loads[3].wait()
+        loads[4].wait()
         xb[m] = jnp.zeros((1, LANES), jnp.float32)
         xb[m, :, pl.ds(0, part)] = (ntv[...] + nsv[...]).reshape(1, part)
 
@@ -176,15 +179,17 @@
     for k in range(3):
         loads[k].wait()
     merge(GATE, 0)
-    norm_part()
+    merge(GATE, 1)
     pl.semaphore_wait(barrier, 3 + models - 1)
     send_own(GATE, 0)
-    norm_exchange()
+    norm_part()
     made = [piece for piece in ORDER if piece[0] != NORM]
-    pending = []
-    for i, piece in enumerate(made[1:]):
+    pending = [(GATE, 1)]
+    for i, piece in enumerate(made[2:]):
+        if i == 1:
+            norm_exchange()
         if piece == (RISE, 0):
-            for k in range(3, 6):
+            for k in range(5, 8):
                 loads[k].wait()
             norm_row()
             pending.insert(0, (NORM, 0))
@@ -222,7 +227,7 @@
         pl.when(core == c)(functools.partial(take, c))
 
 
-def finish_kernel(chips, og, ou, nb, after, lg, lu, ln, send_sem, recv_sem, sib_sem, ready):
+def finish_kernel(chips, og, ou, nb, after, lg, lu, ln, send_sem, recv_sem, sib_sem, moved_sem, ready):
     f, z, core, to, sibling = position(chips)
     before, held = (og, ou, nb), (lg, lu, ln)
     barrier = pltpu.get_barrier_semaphore()
@@ -253,19 +258,38 @@
 
     def hop(source, way, step, kind, p, owner):
         place = ARRIVALS[way].index((step, kind, p))
+        sem = send_sem.at[3, 0] if moved(way, step, kind, p) else send_sem.at[way, kind]
         return copy_to(
             piece_of(source, kind, p, owner), piece_of(held, kind, p, owner),
-            send_sem.at[way, kind], recv_sem.at[way, place], to[way],
-        )
+            sem, recv_sem.at[way, place], to[way],
+        )
+
+    last = chips - 1
+
+    def moved_copy(source, owner):
+        return copy_to(
+            piece_of(source, *MOVED, owner), piece_of(held, *MOVED, owner),
+            moved_sem.at[0], moved_sem.at[1], to[DOWN],
+        )
+
+    def forward(source, way, step, kind, p, owner, sent):
+        if step < HOPS[way][kind]:
+            copy = hop(source, way, step + 1, kind, p, owner)
+            if moved(way, step + 1, kind, p):
+                pl.when(z != last)(copy.start)
+            else:
+                copy.start()
+                sent[way].append((kind, p))
+        elif (kind, p) == MOVED and way == DOWN and step == 3:
+            pl.when(z == 1)(moved_copy(source, owner).start)
 
     def take(c):
         sent = {way: [] for way in (UP, DOWN)}
         pushed, late = [], []
         for i, way, step, kind, p in each(0, FIRST[c]):
             owner = owner_of(chips, z, core, way, step)
-            if step < HOPS[way][kind] and not early(c, way, step + 1, kind, p):
-                hop(before, way, step + 1, kind, p, owner).start()
-                sent[way].append((kind, p))
+            if step == HOPS[way][kind] or not early(c, way, step + 1, kind, p):
+                forward(before, way, step, kind, p, owner, sent)
             if not shared_early(way, i):
                 late.append((before, kind, p, way, step))
 
@@ -283,13 +307,20 @@
             if met:
                 push_late()
             owner = owner_of(chips, z, core, way, step)
-            hop(held, way, step, kind, p, owner).wait_recv()
-            if step < HOPS[way][kind]:
-                hop(held, way, step + 1, kind, p, owner).start()
-                sent[way].append((kind, p))
+            if moved(way, step, kind, p):
+                pl.when(z != 0)(hop(held, way, step, kind, p, owner).wait_recv)
+                pl.when(z == 0)(moved_copy(held, owner).wait_recv)
+            else:
+                hop(held, way, step, kind, p, owner).wait_recv()
+            forward(held, way, step, kind, p, owner, sent)
             late.append((held, kind, p, way, step))
         push_late()
         coming = [(kind, p) for _, _, _, kind, p in each(LEAST, COUNT)]
+        if all(not early(c, UP, 4, *MOVED) for c in (0, 1)):
+            unit = piece_of(held, *MOVED, f)
+            kept = pltpu.make_async_copy(unit, unit, send_sem.at[3, 0])
+            pl.when(z != last)(kept.wait)
+            pl.when(z == 1)(moved_copy(held, f).wait_send)
         for kind in (NORM, GATE, RISE):
             for way in (UP, DOWN):
                 wait_for(held, kind, rows_in(sent[way])[kind], send_sem.at[way, kind])
@@ -388,7 +419,7 @@
             pltpu.VMEM((fsdp, 1, LANES), jnp.float32),
         )
         ring_sems = [
-            pltpu.SemaphoreType.DMA((3, 3)),
+            pltpu.SemaphoreType.DMA((4, 3)),
             pltpu.SemaphoreType.DMA((2, COUNT)),
             pltpu.SemaphoreType.DMA((3,)),
         ]
@@ -427,7 +458,9 @@
             out_shape=on_chip_held,
             in_specs=[on_chip] * 4,
             out_specs=(on_chip,) * 3,
-            scratch_shapes=[*ring_sems, pltpu.SemaphoreType.REGULAR],
+            scratch_shapes=[
+                *ring_sems, pltpu.SemaphoreType.DMA((2,)), pltpu.SemaphoreType.REGULAR
+            ],
             compiler_params=pltpu.CompilerParams(
                 collective_id=1, has_side_effects=True, vmem_limit_bytes=4 << 20
             ),

time: 94 us -> 92.6 us (0.985)
  Pallas kernels: 93.2 us -> 91.8 us
    pallas_call x1, Pallas kernels: 15.4 us -> 11.2 us  [body(): pl.pallas_call(functools.partial(finish_kernel, chips), out_shape=on_chip...]
    pallas_call x1, Pallas kernels: 71.2 us -> 74 us  [body(): pl.pallas_call(functools.partial(gather_kernel, chips), out_shape=on_chip...]
where the time goes in v4:
time: 92.6 us; the launch traced here: 92.5 us
  Pallas kernels  91.8 us (99%)
    pallas_call x1, Pallas kernels, body(): pl.pallas_call(functools.partial(gather_kernel, chips), out_shape=on_chip...  74 us
    pallas_call x1, Pallas kernels, body(): pl.pallas_call(functools.partial(finish_kernel, chips), out_shape=on_chip...  11.2 us
    pallas_call x1, Pallas kernels, body(): pl.pallas_call(functools.partial(write_kernel, chips), out_shape=(final,...  4.84 us

profile of v4, /device:TPU:1, one launch (start us, length us, event | category | flops | bytes accessed | tf_op | source)
XLA Modules:
  0.0 92.5 jit_solution(7722886056047862722)
XLA Ops:
  0.6 74.0 %gather.1 = (bf16[2048,2048]{1,0:T(8,128)(2,1)S(1)}, bf16[2048,2048]{1,0:T(8,128)(2,1)S(1)}, f32[16,1,128]{2,1,0:T(1,128)S(1)}) custom-call(bf16[128,2048]{1,0:T(8,128)(2,1)} %wg.1, bf16[32,128]{1,0:T(8,128)(2,1)} %bitcast.3, bf16[32,2048]{1,0:T(8,128)(2,1)} %hg.1, bf16[128,2048]{1,0:T(8,128)(2,1)} %wu.1, bf16[32,128]{1,0:T(8,128)(2,1)} %bitcast.4, ...), custom_call_target="tpu_custom_call" | custom-call | tf_op jit(solution)/shard_map/gather/pallas_call | solution.py:426
  74.6 4.8 %write.1 = (bf16[2048,2048]{1,0:T(8,128)(2,1)}, bf16[2048,2048]{1,0:T(8,128)(2,1)}, f32[8,128]{1,0:T(8,128)S(1)}) custom-call(bf16[2048,2048]{1,0:T(8,128)(2,1)S(1)} %get-tuple-element.15.og, bf16[2048,2048]{1,0:T(8,128)(2,1)S(1)} %get-tuple-element.16.ou), custom_call_target="tpu_custom_call" | custom-call | tf_op jit(solution)/shard_map/write/pallas_call | solution.py:447
  79.5 11.2 %finish.1 = (bf16[2048,2048]{1,0:T(8,128)(2,1)S(1)}, bf16[2048,2048]{1,0:T(8,128)(2,1)S(1)}, f32[16,1,128]{2,1,0:T(1,128)S(1)}) custom-call(bf16[2048,2048]{1,0:T(8,128)(2,1)S(1)} %get-tuple-element.15.og, bf16[2048,2048]{1,0:T(8,128)(2,1)S(1)} %get-tuple-element.16.ou, f32[16,1,128]{2,1,0:T(1,128)S(1)} %get-tuple-element.19.nb, ...), custom_call_target="tpu_custom_call" | custom-call | tf_op jit(solution)/shard_map/finish/pallas_call | solution.py:456
  90.7 1.8 %write_rest.1 = (bf16[2048,2048]{1,0:T(8,128)(2,1)}, bf16[2048,2048]{1,0:T(8,128)(2,1)}, bf16[16,128]{1,0:T(8,128)(2,1)}) custom-call(bf16[2048,2048]{1,0:T(8,128)(2,1)} %get-tuple-element.17.fg_in, bf16[2048,2048]{1,0:T(8,128)(2,1)} %get-tuple-element.18.fu_in, ...), custom_call_target="tpu_custom_call", output_to_operand_aliasing={{0}: (0, {}), {1}: (1, {})} | custom-call | tf_op jit(solution)/shard_map/write_rest/pallas_call | solution.py:469

commit v5 on v4

--- a/solution.py
+++ b/solution.py
@@ -12,10 +12,10 @@
 UP, DOWN = 0, 1
 GATE, RISE, NORM = 0, 1, 2
 LANES = 128
-CUTS = {GATE: (256, 512, 512, 256, 256, 128, 128), RISE: (512, 512, 512, 256, 128, 128), NORM: (1,)}
+CUTS = {GATE: (256, 512, 512, 128, 384, 128, 128), RISE: (512, 512, 512, 256, 128, 128), NORM: (1,)}
 HOPS = {UP: (4, 3, 4), DOWN: (3, 4, 3)}
 ORDER = [(GATE, p) for p in range(len(CUTS[GATE]))] + [(RISE, p) for p in range(len(CUTS[RISE]))]
-ORDER.insert(3, (NORM, 0))
+ORDER.insert(len(CUTS[GATE]), (NORM, 0))
 ARRIVALS = {
     way: [
         (step, kind, p)
@@ -43,8 +43,8 @@
     f = lax.axis_index("fsdp")
     z, core = f // 2, f % 2
     to = {
-        UP: lax.rem(z + 1, chips) * 2 + core,
-        DOWN: lax.rem(z + chips - 1, chips) * 2 + core,
+        UP: jnp.where(z == chips - 1, 0, z + 1) * 2 + core,
+        DOWN: jnp.where(z == 0, chips - 1, z - 1) * 2 + core,
     }
     return f, z, core, to, z * 2 + (1 - core)
 
@@ -104,17 +104,6 @@
     chips, wg, lg, hg, wu, lu, hu, nt, ns, og, ou, nb,
     wv, lv, hv, ntv, nsv, xb, in_sem, send_sem, recv_sem, sib_sem, x_sem,
 ):
-    loads = []
-    for k, (src, dst) in enumerate(
-        (
-            (lg, lv.at[0]), (hg, hv.at[0]), (wg, wv.at[0]), (nt, ntv), (ns, nsv),
-            (lu, lv.at[1]), (hu, hv.at[1]), (wu, wv.at[1]),
-        )
-    ):
-        load = pltpu.make_async_copy(src, dst, in_sem.at[k])
-        load.start()
-        loads.append(load)
-
     f, z, core, to, sibling = position(chips)
     m = lax.axis_index("model")
     models = lax.axis_size("model")
@@ -124,10 +113,22 @@
         pl.semaphore_signal(
             barrier, inc=1, device_id={"fsdp": peer}, device_id_type=MESH
         )
-    for k in range(1, models):
+    right, left = lax.rem(m + 1, models), lax.rem(m + models - 1, models)
+    for peer in (right, left):
         pl.semaphore_signal(
-            barrier, inc=1, device_id={"model": lax.rem(m + k, models)}, device_id_type=MESH
-        )
+            barrier, inc=1, device_id={"model": peer}, device_id_type=MESH
+        )
+
+    loads = []
+    for k, (src, dst) in enumerate(
+        (
+            (lg, lv.at[0]), (hg, hv.at[0]), (wg, wv.at[0]), (nt, ntv), (ns, nsv),
+            (lu, lv.at[1]), (hu, hv.at[1]), (wu, wv.at[1]),
+        )
+    ):
+        load = pltpu.make_async_copy(src, dst, in_sem.at[k])
+        load.start()
+        loads.append(load)
 
     def push(kind, p, owner):
         ref = piece_of(held, kind, p, owner)
@@ -162,15 +163,16 @@
         xb[m] = jnp.zeros((1, LANES), jnp.float32)
         xb[m, :, pl.ds(0, part)] = (ntv[...] + nsv[...]).reshape(1, part)
 
-    def norm_exchange():
-        for k in range(1, models):
-            pltpu.make_async_remote_copy(
-                src_ref=xb.at[m], dst_ref=xb.at[m], send_sem=x_sem.at[0], recv_sem=x_sem.at[1],
-                device_id={"model": lax.rem(m + k, models)}, device_id_type=MESH,
-            ).start()
+    def norm_send(owner, peer, k):
+        pltpu.make_async_remote_copy(
+            src_ref=xb.at[owner], dst_ref=xb.at[owner], send_sem=x_sem.at[0], recv_sem=x_sem.at[k],
+            device_id={"model": peer}, device_id_type=MESH,
+        ).start()
+
+    def norm_arrived(k):
+        pltpu.make_async_copy(xb.at[0], xb.at[0], x_sem.at[k]).wait()
 
     def norm_row():
-        pltpu.make_async_copy(others, others, x_sem.at[1]).wait()
         row = xb[0]
         for k in range(1, models):
             row = jnp.where(lane >= k * part, pltpu.roll(xb[k], k * part, 1), row)
@@ -179,31 +181,37 @@
     for k in range(3):
         loads[k].wait()
     merge(GATE, 0)
+    norm_part()
     merge(GATE, 1)
-    pl.semaphore_wait(barrier, 3 + models - 1)
+    pl.semaphore_wait(barrier, 5)
+    norm_send(m, left, 1)
+    norm_send(m, right, 2)
     send_own(GATE, 0)
-    norm_part()
-    made = [piece for piece in ORDER if piece[0] != NORM]
-    pending = [(GATE, 1)]
-    for i, piece in enumerate(made[2:]):
-        if i == 1:
-            norm_exchange()
-        if piece == (RISE, 0):
-            for k in range(5, 8):
-                loads[k].wait()
-            norm_row()
-            pending.insert(0, (NORM, 0))
-        merge(*piece)
-        pending.append(piece)
-        if piece[0] == GATE and piece[1] < 3:
-            if len(pending) > 1:
-                send_own(*pending.pop(0))
-        elif piece[0] == RISE:
-            while len(pending) > 1:
-                send_own(*pending.pop(0))
+    merge(GATE, 2)
+    send_own(GATE, 1)
+    merge(GATE, 3)
+    send_own(GATE, 2)
+    for p in range(4, len(CUTS[GATE])):
+        merge(GATE, p)
+        send_own(GATE, p - 1)
+    for k in range(5, 8):
+        loads[k].wait()
+    merge(RISE, 0)
+    send_own(GATE, len(CUTS[GATE]) - 1)
+    merge(RISE, 1)
+    for k in range(2, models - 1):
+        norm_arrived(k)
+        norm_send(lax.rem(m + models + 1 - k, models), right, k + 1)
+    merge(RISE, 2)
+    merge(RISE, 3)
+    norm_arrived(1)
+    norm_arrived(models - 1)
+    norm_row()
+    for p in range(4, len(CUTS[RISE])):
+        merge(RISE, p)
+    for piece in ORDER[len(CUTS[GATE]) :]:
+        send_own(*piece)
     pltpu.make_async_copy(others, others, x_sem.at[0]).wait()
-    while pending:
-        send_own(*pending.pop(0))
 
     def take(c):
         sent = {way: list(ORDER) for way in (UP, DOWN)}
@@ -344,7 +352,7 @@
 
 def store(chips, z, core, c, held, final, sem, sides, own):
     total = [0, 0]
-    for mine, (first, last) in ((True, sides[0]), (False, sides[1])):
+    for mine, (first, last) in ((False, sides[1]), (True, sides[0])):
         line = core if mine else 1 - core
         blocks = {}
         for _, way, step, kind, p in each(first, last):
@@ -437,7 +445,7 @@
                 pltpu.VMEM((models, 1, LANES), jnp.float32),
                 pltpu.SemaphoreType.DMA((8,)),
                 *ring_sems,
-                pltpu.SemaphoreType.DMA((2,)),
+                pltpu.SemaphoreType.DMA((models,)),
             ],
             compiler_params=pltpu.CompilerParams(
                 collective_id=0, has_side_effects=True, vmem_limit_bytes=50257920

time: 92.6 us -> 92.1 us (level)
  no operation moved by 1% of the time
where the time goes in v5:
time: 92.1 us; the launch traced here: 92 us
  Pallas kernels  91.3 us (99%)
    pallas_call x1, Pallas kernels, body(): pl.pallas_call(functools.partial(gather_kernel, chips), out_shape=on_chip...  73.7 us
    pallas_call x1, Pallas kernels, body(): pl.pallas_call(functools.partial(finish_kernel, chips), out_shape=on_chip...  11 us
    pallas_call x1, Pallas kernels, body(): pl.pallas_call(functools.partial(write_kernel, chips), out_shape=(final,...  4.84 us

profile of v5, /device:TPU:1, one launch (start us, length us, event | category | flops | bytes accessed | tf_op | source)
XLA Modules:
  0.0 92.0 jit_solution(14936358427089876094)
XLA Ops:
  0.6 73.7 %gather.1 = (bf16[2048,2048]{1,0:T(8,128)(2,1)S(1)}, bf16[2048,2048]{1,0:T(8,128)(2,1)S(1)}, f32[16,1,128]{2,1,0:T(1,128)S(1)}) custom-call(bf16[128,2048]{1,0:T(8,128)(2,1)} %wg.1, bf16[32,128]{1,0:T(8,128)(2,1)} %bitcast.3, bf16[32,2048]{1,0:T(8,128)(2,1)} %hg.1, bf16[128,2048]{1,0:T(8,128)(2,1)} %wu.1, bf16[32,128]{1,0:T(8,128)(2,1)} %bitcast.4, ...), custom_call_target="tpu_custom_call" | custom-call | tf_op jit(solution)/shard_map/gather/pallas_call | solution.py:434
  74.3 4.8 %write.1 = (bf16[2048,2048]{1,0:T(8,128)(2,1)}, bf16[2048,2048]{1,0:T(8,128)(2,1)}, f32[8,128]{1,0:T(8,128)S(1)}) custom-call(bf16[2048,2048]{1,0:T(8,128)(2,1)S(1)} %get-tuple-element.15.og, bf16[2048,2048]{1,0:T(8,128)(2,1)S(1)} %get-tuple-element.16.ou), custom_call_target="tpu_custom_call" | custom-call | tf_op jit(solution)/shard_map/write/pallas_call | solution.py:455
  79.2 11.0 %finish.1 = (bf16[2048,2048]{1,0:T(8,128)(2,1)S(1)}, bf16[2048,2048]{1,0:T(8,128)(2,1)S(1)}, f32[16,1,128]{2,1,0:T(1,128)S(1)}) custom-call(bf16[2048,2048]{1,0:T(8,128)(2,1)S(1)} %get-tuple-element.15.og, bf16[2048,2048]{1,0:T(8,128)(2,1)S(1)} %get-tuple-element.16.ou, f32[16,1,128]{2,1,0:T(1,128)S(1)} %get-tuple-element.19.nb, ...), custom_call_target="tpu_custom_call" | custom-call | tf_op jit(solution)/shard_map/finish/pallas_call | solution.py:464
  90.2 1.8 %write_rest.1 = (bf16[2048,2048]{1,0:T(8,128)(2,1)}, bf16[2048,2048]{1,0:T(8,128)(2,1)}, bf16[16,128]{1,0:T(8,128)(2,1)}) custom-call(bf16[2048,2048]{1,0:T(8,128)(2,1)} %get-tuple-element.17.fg_in, bf16[2048,2048]{1,0:T(8,128)(2,1)} %get-tuple-element.18.fu_in, ...), custom_call_target="tpu_custom_call", output_to_operand_aliasing={{0}: (0, {}), {1}: (1, {})} | custom-call | tf_op jit(solution)/shard_map/write_rest/pallas_call | solution.py:477

commit v6 on v5

--- a/solution.py
+++ b/solution.py
@@ -1,4 +1,5 @@
 import functools
+import itertools
 
 import jax
 import jax.numpy as jnp
@@ -14,13 +15,17 @@
 LANES = 128
 CUTS = {GATE: (256, 512, 512, 128, 384, 128, 128), RISE: (512, 512, 512, 256, 128, 128), NORM: (1,)}
 HOPS = {UP: (4, 3, 4), DOWN: (3, 4, 3)}
-ORDER = [(GATE, p) for p in range(len(CUTS[GATE]))] + [(RISE, p) for p in range(len(CUTS[RISE]))]
-ORDER.insert(len(CUTS[GATE]), (NORM, 0))
+BLOCK = {kind: [(kind, p) for p in range(len(CUTS[kind]))] for kind in (GATE, RISE, NORM)}
+ORDERS = {
+    UP: BLOCK[GATE] + BLOCK[NORM] + BLOCK[RISE],
+    DOWN: BLOCK[RISE] + BLOCK[NORM] + BLOCK[GATE],
+}
+ORDER = ORDERS[UP]
 ARRIVALS = {
     way: [
         (step, kind, p)
         for step in range(1, 5)
-        for kind, p in ORDER
+        for kind, p in ORDERS[way]
         if step <= HOPS[way][kind]
     ]
     for way in (UP, DOWN)
@@ -28,7 +33,7 @@
 FIRST = (29, 45)
 LEAST = min(FIRST)
 AHEAD = FIRST.index(LEAST)
-MEET = 39
+MEET = 41
 
 
 def early(core, way, step, kind, p):
@@ -139,10 +144,8 @@
         place = ARRIVALS[way].index((step, kind, p))
         return copy_to(ref, ref, send_sem.at[way, kind], recv_sem.at[way, place], to[way])
 
-    def send_own(kind, p):
-        for way in (UP, DOWN):
-            hop(way, 1, kind, p, f).start()
-        push(kind, p, f)
+    def send_own(way, kind, p):
+        hop(way, 1, kind, p, f).start()
 
     def merge(kind, p):
         columns = rows_of(kind, p)
@@ -178,39 +181,47 @@
             row = jnp.where(lane >= k * part, pltpu.roll(xb[k], k * part, 1), row)
         nb[f] = row
 
-    for k in range(3):
+    made = [
+        piece
+        for pair in itertools.zip_longest(BLOCK[GATE], BLOCK[RISE])
+        for piece in pair
+        if piece
+    ]
+
+    def first_send(kind, p):
+        send_own(UP if kind == GATE else DOWN, kind, p)
+        push(kind, p, f)
+
+    for k in (0, 1, 2):
         loads[k].wait()
-    merge(GATE, 0)
+    merge(*made[0])
     norm_part()
-    merge(GATE, 1)
+    for k in (5, 6, 7):
+        loads[k].wait()
+    merge(*made[1])
+    merge(*made[2])
     pl.semaphore_wait(barrier, 5)
     norm_send(m, left, 1)
     norm_send(m, right, 2)
-    send_own(GATE, 0)
-    merge(GATE, 2)
-    send_own(GATE, 1)
-    merge(GATE, 3)
-    send_own(GATE, 2)
-    for p in range(4, len(CUTS[GATE])):
-        merge(GATE, p)
-        send_own(GATE, p - 1)
-    for k in range(5, 8):
-        loads[k].wait()
-    merge(RISE, 0)
-    send_own(GATE, len(CUTS[GATE]) - 1)
-    merge(RISE, 1)
+    first_send(*made[0])
+    first_send(*made[1])
+    for before, piece in zip(made[2:], made[3:]):
+        merge(*piece)
+        first_send(*before)
     for k in range(2, models - 1):
         norm_arrived(k)
         norm_send(lax.rem(m + models + 1 - k, models), right, k + 1)
-    merge(RISE, 2)
-    merge(RISE, 3)
+    first_send(*made[-1])
     norm_arrived(1)
     norm_arrived(models - 1)
     norm_row()
-    for p in range(4, len(CUTS[RISE])):
-        merge(RISE, p)
-    for piece in ORDER[len(CUTS[GATE]) :]:
-        send_own(*piece)
+    for way, kind in ((UP, RISE), (DOWN, GATE)):
+        send_own(way, *BLOCK[kind][0])
+        if way == UP:
+            push(NORM, 0, f)
+        send_own(way, NORM, 0)
+        for piece in BLOCK[kind][1:]:
+            send_own(way, *piece)
     pltpu.make_async_copy(others, others, x_sem.at[0]).wait()
 
     def take(c):

time: 92.1 us -> 92.1 us (level)
  no operation moved by 1% of the time
where the time goes in v6:
time: 92.1 us; the launch traced here: 92 us
  Pallas kernels  91.3 us (99%)
    pallas_call x1, Pallas kernels, body(): pl.pallas_call(functools.partial(gather_kernel, chips), out_shape=on_chip...  73.5 us
    pallas_call x1, Pallas kernels, body(): pl.pallas_call(functools.partial(finish_kernel, chips), out_shape=on_chip...  11.3 us
    pallas_call x1, Pallas kernels, body(): pl.pallas_call(functools.partial(write_kernel, chips), out_shape=(final,...  4.86 us

profile of v6, /device:TPU:1, one launch (start us, length us, event | category | flops | bytes accessed | tf_op | source)
XLA Modules:
  0.0 92.0 jit_solution(1427012614087229621)
XLA Ops:
  0.6 73.5 %gather.1 = (bf16[2048,2048]{1,0:T(8,128)(2,1)S(1)}, bf16[2048,2048]{1,0:T(8,128)(2,1)S(1)}, f32[16,1,128]{2,1,0:T(1,128)S(1)}) custom-call(bf16[128,2048]{1,0:T(8,128)(2,1)} %wg.1, bf16[32,128]{1,0:T(8,128)(2,1)} %bitcast.3, bf16[32,2048]{1,0:T(8,128)(2,1)} %hg.1, bf16[128,2048]{1,0:T(8,128)(2,1)} %wu.1, bf16[32,128]{1,0:T(8,128)(2,1)} %bitcast.4, ...), custom_call_target="tpu_custom_call" | custom-call | tf_op jit(solution)/shard_map/gather/pallas_call | solution.py:445
  74.1 4.9 %write.1 = (bf16[2048,2048]{1,0:T(8,128)(2,1)}, bf16[2048,2048]{1,0:T(8,128)(2,1)}, f32[8,128]{1,0:T(8,128)S(1)}) custom-call(bf16[2048,2048]{1,0:T(8,128)(2,1)S(1)} %get-tuple-element.15.og, bf16[2048,2048]{1,0:T(8,128)(2,1)S(1)} %get-tuple-element.16.ou), custom_call_target="tpu_custom_call" | custom-call | tf_op jit(solution)/shard_map/write/pallas_call | solution.py:466
  79.0 11.3 %finish.1 = (bf16[2048,2048]{1,0:T(8,128)(2,1)S(1)}, bf16[2048,2048]{1,0:T(8,128)(2,1)S(1)}, f32[16,1,128]{2,1,0:T(1,128)S(1)}) custom-call(bf16[2048,2048]{1,0:T(8,128)(2,1)S(1)} %get-tuple-element.15.og, bf16[2048,2048]{1,0:T(8,128)(2,1)S(1)} %get-tuple-element.16.ou, f32[16,1,128]{2,1,0:T(1,128)S(1)} %get-tuple-element.19.nb, ...), custom_call_target="tpu_custom_call" | custom-call | tf_op jit(solution)/shard_map/finish/pallas_call | solution.py:475
  90.2 1.8 %write_rest.1 = (bf16[2048,2048]{1,0:T(8,128)(2,1)}, bf16[2048,2048]{1,0:T(8,128)(2,1)}, bf16[16,128]{1,0:T(8,128)(2,1)}) custom-call(bf16[2048,2048]{1,0:T(8,128)(2,1)} %get-tuple-element.17.fg_in, bf16[2048,2048]{1,0:T(8,128)(2,1)} %get-tuple-element.18.fu_in, ...), custom_call_target="tpu_custom_call", output_to_operand_aliasing={{0}: (0, {}), {1}: (1, {})} | custom-call | tf_op jit(solution)/shard_map/write_rest/pallas_call | solution.py:488

commit v7 on v6

--- a/solution.py
+++ b/solution.py
@@ -30,7 +30,7 @@
     ]
     for way in (UP, DOWN)
 }
-FIRST = (29, 45)
+FIRST = (29, 46)
 LEAST = min(FIRST)
 AHEAD = FIRST.index(LEAST)
 MEET = 41

time: 92.1 us -> 92.1 us (level)
  no operation moved by 1% of the time
where the time goes in v7:
time: 92.1 us; the launch traced here: 92 us
  Pallas kernels  91.3 us (99%)
    pallas_call x1, Pallas kernels, body(): pl.pallas_call(functools.partial(gather_kernel, chips), out_shape=on_chip...  74.2 us
    pallas_call x1, Pallas kernels, body(): pl.pallas_call(functools.partial(finish_kernel, chips), out_shape=on_chip...  10.5 us
    pallas_call x1, Pallas kernels, body(): pl.pallas_call(functools.partial(write_kernel, chips), out_shape=(final,...  4.89 us

profile of v7, /device:TPU:1, one launch (start us, length us, event | category | flops | bytes accessed | tf_op | source)
XLA Modules:
  0.0 92.0 jit_solution(16147657205602356740)
XLA Ops:
  0.6 74.2 %gather.1 = (bf16[2048,2048]{1,0:T(8,128)(2,1)S(1)}, bf16[2048,2048]{1,0:T(8,128)(2,1)S(1)}, f32[16,1,128]{2,1,0:T(1,128)S(1)}) custom-call(bf16[128,2048]{1,0:T(8,128)(2,1)} %wg.1, bf16[32,128]{1,0:T(8,128)(2,1)} %bitcast.3, bf16[32,2048]{1,0:T(8,128)(2,1)} %hg.1, bf16[128,2048]{1,0:T(8,128)(2,1)} %wu.1, bf16[32,128]{1,0:T(8,128)(2,1)} %bitcast.4, ...), custom_call_target="tpu_custom_call" | custom-call | tf_op jit(solution)/shard_map/gather/pallas_call | solution.py:445
  74.8 4.9 %write.1 = (bf16[2048,2048]{1,0:T(8,128)(2,1)}, bf16[2048,2048]{1,0:T(8,128)(2,1)}, f32[8,128]{1,0:T(8,128)S(1)}) custom-call(bf16[2048,2048]{1,0:T(8,128)(2,1)S(1)} %get-tuple-element.15.og, bf16[2048,2048]{1,0:T(8,128)(2,1)S(1)} %get-tuple-element.16.ou), custom_call_target="tpu_custom_call" | custom-call | tf_op jit(solution)/shard_map/write/pallas_call | solution.py:466
  79.7 10.5 %finish.1 = (bf16[2048,2048]{1,0:T(8,128)(2,1)S(1)}, bf16[2048,2048]{1,0:T(8,128)(2,1)S(1)}, f32[16,1,128]{2,1,0:T(1,128)S(1)}) custom-call(bf16[2048,2048]{1,0:T(8,128)(2,1)S(1)} %get-tuple-element.15.og, bf16[2048,2048]{1,0:T(8,128)(2,1)S(1)} %get-tuple-element.16.ou, f32[16,1,128]{2,1,0:T(1,128)S(1)} %get-tuple-element.19.nb, ...), custom_call_target="tpu_custom_call" | custom-call | tf_op jit(solution)/shard_map/finish/pallas_call | solution.py:475
  90.2 1.7 %write_rest.1 = (bf16[2048,2048]{1,0:T(8,128)(2,1)}, bf16[2048,2048]{1,0:T(8,128)(2,1)}, bf16[16,128]{1,0:T(8,128)(2,1)}) custom-call(bf16[2048,2048]{1,0:T(8,128)(2,1)} %get-tuple-element.17.fg_in, bf16[2048,2048]{1,0:T(8,128)(2,1)} %get-tuple-element.18.fu_in, ...), custom_call_target="tpu_custom_call", output_to_operand_aliasing={{0}: (0, {}), {1}: (1, {})} | custom-call | tf_op jit(solution)/shard_map/write_rest/pallas_call | solution.py:488
